TPU v7x, 32 devices: a whole 2x2x4 slice. The times are simulated.
32 devices in a mesh: cosmo: 2 (over x), row: 16 (over z, y, core).
Axes of the slice: x: 2, y: 2, z: 4, core: 2. Of those that a mesh axis runs over, the one named last changes fastest.
Arguments:
- potentials: float32 [4, 256, 16384], P('cosmo', 'row'), parts along dimension 0, may hold values from -3 to 3
- ratios: float32 [6], P('cosmo'), parts along dimension 0, may hold values from 0.3 to 0.9
- row_offset: int32 [256], P('cosmo'), parts along dimension 0, may hold values from 0 to 7
- col_offset: int32 [256], P('cosmo'), parts along dimension 0, may hold values from 0 to 127
Outputs:
- convergence: float32 [512, 16384], P(('cosmo', 'row')), parts along dimension 0
- shear_map: float32 [2, 512, 16384], P(None, ('cosmo', 'row')), parts along dimension 1
- rotation: float32 [512, 16384], P(('cosmo', 'row')), parts along dimension 0
- displacement: float32 [2, 512, 16384], P(None, ('cosmo', 'row')), parts along dimension 1
There are 2 independent parts, one for each index of `cosmo`. A program takes and returns all parts, laid end to end along the dimension named above; each array names one. Nothing has to cross between parts.
Inputs may be any that keep to these rules, and one draw needn't show every extreme that they name: `row_offset`: row offsets count blocks of 32 rows.
All inputs are finite; a program needn't handle non-finite values.
Results may differ from a plain program's by a relative error of at most 0.00002.
Values sent between devices are 32-bit elements; how exact they have to be, the bound alone decides.
A program may use at most 128 MiB of HBM per device.

v0:
```python
import jax
import jax.numpy as jnp
from jax import lax
from jax.sharding import PartitionSpec as P

BITS = 3
RB = 8


def with_halo(cells, sides, width):
    for axis, dim in sides:
        count = lax.axis_size(axis)
        head = lax.slice_in_dim(cells, 0, width, axis=dim)
        tail = lax.slice_in_dim(cells, cells.shape[dim] - width, cells.shape[dim], axis=dim)
        cells = jnp.concatenate(
            [
                lax.ppermute(tail, axis, [(i, (i + 1) % count) for i in range(count)]),
                cells,
                lax.ppermute(head, axis, [((i + 1) % count, i) for i in range(count)]),
            ],
            axis=dim,
        )
    return cells


def passed_along(x, axis, by):
    size = lax.axis_size(axis)
    return lax.ppermute(x, axis, [(i, (i + by) % size) for i in range(size)])


def column_slope(field):
    return (
        8.0 * (jnp.roll(field, -1, 2) - jnp.roll(field, 1, 2))
        - (jnp.roll(field, -2, 2) - jnp.roll(field, 2, 2))
    ) / 12.0


def row_slope(padded, height):
    return (
        8.0 * (padded[:, 3 : height + 3] - padded[:, 1 : height + 1])
        - (padded[:, 4 : height + 4] - padded[:, 0:height])
    ) / 12.0


def derive(field):
    height = field.shape[1]
    padded = with_halo(field, (("row", 1),), 2)
    slope_r = row_slope(padded, height)
    slope_rim = with_halo(slope_r, (("row", 1),), 2)
    curve_rr = row_slope(slope_rim, height)
    slope_c = column_slope(field)
    return (slope_r, slope_c, curve_rr, column_slope(slope_r), column_slope(slope_c))


def assemble(nearer, farther, ratios):
    near_r, near_c, near_rr, near_rc, near_cc = nearer
    far_r, far_c, far_rr, far_rc, far_cc = farther
    beta_near = ratios[0]
    beta_one = ratios[1]
    beta_two = ratios[2]
    inner_rr = 1.0 - beta_near * near_rr
    inner_rc = -beta_near * near_rc
    inner_cc = 1.0 - beta_near * near_cc
    chain_rr = far_rr * inner_rr + far_rc * inner_rc
    chain_rc = far_rr * inner_rc + far_rc * inner_cc
    chain_cr = far_rc * inner_rr + far_cc * inner_rc
    chain_cc = far_rc * inner_rc + far_cc * inner_cc
    total_rr = 1.0 - beta_one * near_rr - beta_two * chain_rr
    total_rc = -beta_one * near_rc - beta_two * chain_rc
    total_cr = -beta_one * near_rc - beta_two * chain_cr
    total_cc = 1.0 - beta_one * near_cc - beta_two * chain_cc
    convergence = 1.0 - 0.5 * (total_rr + total_cc)
    shear_map = jnp.stack([0.5 * (total_rr - total_cc), -0.5 * (total_rc + total_cr)])
    rotation = 0.5 * (total_rc - total_cr)
    displacement = jnp.stack(
        [beta_one * near_r + beta_two * far_r, beta_one * near_c + beta_two * far_c]
    )
    return (convergence, shear_map, rotation, displacement)


def per_device(potentials, ratios, row_offset, col_offset):
    devices = lax.axis_size("row")
    height = potentials.shape[1]
    columns = potentials.shape[2]
    blocks = columns // 128
    source = (jnp.arange(blocks, dtype=jnp.int32) + col_offset) % blocks
    stride = devices // RB
    fields = derive(potentials[0:1])
    nearer = tuple((member[0] for member in fields))
    strips = potentials[1].reshape(height, blocks, 128)
    left_part = jnp.take(strips, (source - 1) % blocks, axis=1)[:, :, 64:]
    middle_part = jnp.take(strips, source, axis=1)
    right_part = jnp.take(strips, (source + 1) % blocks, axis=1)[:, :, :64]
    windows = jnp.concatenate([left_part, middle_part, right_part], axis=2)
    for bit_level in range(BITS):
        arrived = passed_along(windows, "row", devices - stride * 2**bit_level)
        picked = (row_offset // 2**bit_level % 2 == 1).reshape(1, blocks, 1)
        windows = jnp.where(picked, arrived, windows)
    derived = derive(windows.reshape(1, height, blocks * 256))
    farther = tuple(
        (
            member[0].reshape(height, blocks, 256)[:, :, 64:192].reshape(height, columns)
            for member in derived
        )
    )
    return assemble(nearer, farther, ratios)


def solution(mesh):
    return jax.shard_map(
        per_device,
        mesh=mesh,
        in_specs=(P("cosmo", "row", None), P("cosmo"), P("cosmo"), P("cosmo")),
        out_specs=(
            P(("cosmo", "row"), None),
            P(None, ("cosmo", "row"), None),
            P(("cosmo", "row"), None),
            P(None, ("cosmo", "row"), None),
        ),
        check_vma=False,
    )
```

profile of v0, /device:TPU:0, one launch (start us, length us, event | category | flops | bytes accessed | tf_op | source)
XLA Modules:
  0.0 314.2 jit_solution(12273258720987648040)
XLA Ops:
  1.3 2.6 fusion.81
  11.1 6.1 %collective-permute-start.4 = (f32[16,128,256]{2,0,1:T(8,128)S(1)}, f32[16,128,256]{2,0,1:T(8,128)S(1)}, u32[]{:S(2)}, u32[]{:S(2)}) collective-permute-start(f32[16,128,256]{2,0,1:T(8,128)S(1)} %pad_maximum_fusion.3), channel_id=1, source_target_pairs={{0,14},{1,15},{2,0},{3,1},{4,2},{5,3},{6,4},{7,5},{8,6},{9,7},{10,... | collective-permute-start | bytes 6291464 | tf_op jit(solution)/shard_map/ppermute | solution.py:28
  18.0 4.4 %collective-permute-start = (f32[1,2,16384]{2,1,0:T(2,128)}, f32[1,2,16384]{2,1,0:T(2,128)}, u32[]{:S(2)}, u32[]{:S(2)}) collective-permute-start(f32[1,2,16384]{2,1,0:T(2,128)} %get-tuple-element.29), channel_id=1, source_target_pairs={{1,0},{2,1},{3,2},{4,3},{5,4},{6,5},{7,6},{8,7},{9,8},{10,9},{11,1... | collective-permute-start | bytes 393224 | tf_op jit(solution)/shard_map/ppermute | solution.py:19
  25.8 36.3 %collective-permute-done.4 = f32[16,128,256]{2,0,1:T(8,128)S(1)} collective-permute-done((f32[16,128,256]{2,0,1:T(8,128)S(1)}, f32[16,128,256]{2,0,1:T(8,128)S(1)}, u32[]{:S(2)}, u32[]{:S(2)}) %collective-permute-start.4) | collective-permute-done | bytes 2097184 | tf_op jit(solution)/shard_map/ppermute | solution.py:28
  63.1 3.2 %collective-permute-start.5 = (f32[16,128,256]{2,0,1:T(8,128)S(1)}, f32[16,128,256]{2,0,1:T(8,128)S(1)}, u32[]{:S(2)}, u32[]{:S(2)}) collective-permute-start(f32[16,128,256]{2,0,1:T(8,128)S(1)} %broadcast_select_fusion), channel_id=1, source_target_pairs={{0,12},{1,13},{2,14},{3,15},{4,0},{5,1},{6,2},{7,3},{8,4},{9,5},{1... | collective-permute-start | bytes 6291464 | tf_op jit(solution)/shard_map/ppermute | solution.py:28
  68.1 42.3 %collective-permute-done.5 = f32[16,128,256]{2,0,1:T(8,128)S(1)} collective-permute-done((f32[16,128,256]{2,0,1:T(8,128)S(1)}, f32[16,128,256]{2,0,1:T(8,128)S(1)}, u32[]{:S(2)}, u32[]{:S(2)}) %collective-permute-start.5) | collective-permute-done | bytes 2097184 | tf_op jit(solution)/shard_map/ppermute | solution.py:28
  113.8 88.4 %collective-permute-done.6 = f32[16,128,256]{2,0,1:T(8,128)S(1)} collective-permute-done((f32[16,128,256]{2,0,1:T(8,128)S(1)}, f32[16,128,256]{2,0,1:T(8,128)S(1)}, u32[]{:S(2)}, u32[]{:S(2)}) %collective-permute-start.6) | collective-permute-done | bytes 2097184 | tf_op jit(solution)/shard_map/ppermute | solution.py:28
  202.5 2.5 copy.35
  209.5 2.7 fusion.91
  212.2 2.7 fusion.89
  220.0 4.1 %multiply_add_fusion = (f32[1,16,16384]{2,1,0:T(8,128)}, f32[1,16,16384]{2,1,0:T(8,128)S(1)}) fusion(f32[1,16,16384]{2,1,0:T(8,128)} %mul.474, f32[]{:T(128)} %bitcast, f32[1,16,16382]{2,1,0:T(8,128)} %get-tuple-element.26, f32[1,16,2]{2,1,0:T(8,128)S(1)} %get-tuple-element.28, f32[1,16,2]{2,1,0:T(8,128)S(1)} %get-tuple-element.27, ...), kind=kLoop, calls=%fused_computation.116 | loop fusion | flops 2621440 | bytes 7340036 | tf_op jit(solution)/shard_map/add | solution.py:76
  224.2 2.5 fusion.102
  226.7 2.5 fusion.100
  229.2 4.2 %collective-permute-start.7 = (f32[1,2,32768]{2,1,0:T(2,128)}, f32[1,2,32768]{2,1,0:T(2,128)}, u32[]{:S(2)}, u32[]{:S(2)}) collective-permute-start(f32[1,2,32768]{2,1,0:T(2,128)} %get-tuple-element.43), channel_id=1, source_target_pairs={{1,0},{2,1},{3,2},{4,3},{5,4},{6,5},{7,6},{8,7},{9,8},{10,9},{11,1... | collective-permute-start | bytes 786440 | tf_op jit(solution)/shard_map/ppermute | solution.py:19
  237.2 2.5 reshape.1144
  240.4 1.8 constant_dynamic-update-slice_fusion
  242.2 3.8 %collective-permute-done.8 = f32[1,2,32768]{2,1,0:T(2,128)S(1)} collective-permute-done((f32[1,2,32768]{2,1,0:T(2,128)}, f32[1,2,32768]{2,1,0:T(2,128)S(1)}, u32[]{:S(2)}, u32[]{:S(2)}) %collective-permute-start.8) | collective-permute-done | bytes 262176 | tf_op jit(solution)/shard_map/ppermute | solution.py:17
  245.9 3.9 %fusion.10 = f32[1,16,32768]{2,1,0:T(8,128)S(1)} fusion(f32[1,2,32768]{2,1,0:T(2,128)S(1)} %collective-permute-done.8, f32[1,16,32768]{2,1,0:T(8,128)S(1)} %reshape.1138, f32[1,18,32768]{2,1,0:T(8,128)} %constant_dynamic-update-slice_fusion), kind=kLoop, calls=%fused_computation.19 | loop fusion | flops 3670016 | bytes 8650752 | tf_op jit(solution)/shard_map/div | solution.py:39
  250.7 2.7 fusion.86
  253.3 2.7 fusion.84
  257.6 2.0 slice_multiply_fusion.1
  261.1 3.4 %multiply_add_fusion.1 = (f32[1,16,16384]{2,1,0:T(8,128)S(1)}, f32[1,16,16384]{2,1,0:T(8,128)S(1)}) fusion(f32[1,16,16384]{2,1,0:T(8,128)S(1)} %mul.471, f32[]{:T(128)} %bitcast, f32[1,16,16384]{2,1,0:T(8,128)} %get-tuple-element.31, f32[1,2,16384]{2,1,0:T(2,128)S(1)} %collective-permute-done.1, f32[1,2,16384]{2,1,0:T(2,128)} %collective-permute-done), kind=kLoop, calls=%fused_computation.117 | loop fusion | flops 2621440 | bytes 4456452 | tf_op jit(solution)/shard_map/add | solution.py:76
  265.4 2.4 fusion.98
  267.8 2.5 fusion.96
  270.4 4.4 %collective-permute-start.9 = (f32[1,2,32768]{2,1,0:T(2,128)}, f32[1,2,32768]{2,1,0:T(2,128)}, u32[]{:S(2)}, u32[]{:S(2)}) collective-permute-start(f32[1,2,32768]{2,1,0:T(2,128)} %get-tuple-element.33), channel_id=1, source_target_pairs={{1,0},{2,1},{3,2},{4,3},{5,4},{6,5},{7,6},{8,7},{9,8},{10,9},{11,1... | collective-permute-start | bytes 786440 | tf_op jit(solution)/shard_map/ppermute | solution.py:19
  274.8 4.4 %collective-permute-start.2 = (f32[1,2,16384]{2,1,0:T(2,128)}, f32[1,2,16384]{2,1,0:T(2,128)}, u32[]{:S(2)}, u32[]{:S(2)}) collective-permute-start(f32[1,2,16384]{2,1,0:T(2,128)} %get-tuple-element.93), channel_id=1, source_target_pairs={{1,0},{2,1},{3,2},{4,3},{5,4},{6,5},{7,6},{8,7},{9,8},{10,9},{11,1... | collective-permute-start | bytes 393224 | tf_op jit(solution)/shard_map/ppermute | solution.py:19
  286.0 2.4 reshape.1143
  289.1 2.4 fusion.4
  293.6 2.4 reshape.1142
  296.1 8.7 %fusion.42 = (f32[16,16384]{1,0:T(8,128)}, f32[1,16,16384]{2,1,0:T(8,128)S(1)}, f32[16,16384]{1,0:T(8,128)S(1)}, f32[16,16384]{1,0:T(8,128)S(1)}) fusion(f32[2,8,128,128]{3,2,1,0:T(8,128)S(1)} %bitcast.127, f32[2,8,128,128]{3,2,1,0:T(8,128)S(1)} %bitcast.129, f32[2,8,128,128]{3,2,1,0:T(8,128)} %bitcast.131, f32[]{:T(128)} %bitcast.25, f32[]{:T(128)} %bitcast.6, ...), kind=kLoop, calls=%fused_computation.73 | loop fusion | flops 11010048 | bytes 17042688 | tf_op jit(solution)/shard_map/mul | solution.py:74
  304.9 4.0 %fusion.37 = f32[16,16384]{1,0:T(8,128)} fusion(f32[16,16384]{1,0:T(8,128)S(1)} %get-tuple-element.12, f32[2,8,128,128]{3,2,1,0:T(8,128)S(1)} %bitcast.128, f32[2,8,128,128]{3,2,1,0:T(8,128)S(1)} %bitcast.130, f32[2,8,128,128]{3,2,1,0:T(8,128)S(1)} %bitcast.132, f32[16,16384]{1,0:T(8,128)S(1)} %get-tuple-element.11, ...), kind=kLoop, calls=%fused_computation.68 | loop fusion | flops 5505024 | bytes 7340048 | tf_op jit(solution)/shard_map/sub | solution.py:72
  309.0 2.5 subtract_multiply_fusion
  (161 shorter events, 46.9 us)
Async XLA Ops:
  10.2 7.0 %copy-start.2 = (f32[2,16,16384]{2,1,0:T(8,128)S(1)}, f32[2,16,16384]{2,1,0:T(8,128)}, u32[]{:S(2)}) copy-start(f32[2,16,16384]{2,1,0:T(8,128)} %param.6) | copy-start | bytes 6291460
  10.2 12.2 %copy-start.42 = (f32[3]{0:T(128)S(1)}, f32[3]{0:T(128)}, u32[]{:S(2)}) copy-start(f32[3]{0:T(128)} %param.7) | copy-start | bytes 40
  10.3 15.4 %copy-start.43 = (s32[128]{0:T(128)S(1)}, s32[128]{0:T(128)}, u32[]{:S(2)}) copy-start(s32[128]{0:T(128)} %param.8) | copy-start | bytes 1540
  11.1 51.0 %collective-permute-start.4 = (f32[16,128,256]{2,0,1:T(8,128)S(1)}, f32[16,128,256]{2,0,1:T(8,128)S(1)}, u32[]{:S(2)}, u32[]{:S(2)}) collective-permute-start(f32[16,128,256]{2,0,1:T(8,128)S(1)} %pad_maximum_fusion.3), channel_id=1, source_target_pairs={{0,14},{1,15},{2,0},{3,1},{4,2},{5,3},{6,4},{7,5},{8,6},{9,7},{10,... | collective-permute-start | bytes 6291464 | tf_op jit(solution)/shard_map/ppermute | solution.py:28
  18.0 243.1 %collective-permute-start.1 = (f32[1,2,16384]{2,1,0:T(2,128)}, f32[1,2,16384]{2,1,0:T(2,128)S(1)}, u32[]{:S(2)}, u32[]{:S(2)}) collective-permute-start(f32[1,2,16384]{2,1,0:T(2,128)} %get-tuple-element.30), channel_id=1, source_target_pairs={{0,1},{1,2},{2,3},{3,4},{4,5},{5,6},{6,7},{7,8},{8,9},{9,10},{10,1... | collective-permute-start | bytes 393224 | tf_op jit(solution)/shard_map/ppermute | solution.py:17
  18.0 243.1 %collective-permute-start = (f32[1,2,16384]{2,1,0:T(2,128)}, f32[1,2,16384]{2,1,0:T(2,128)}, u32[]{:S(2)}, u32[]{:S(2)}) collective-permute-start(f32[1,2,16384]{2,1,0:T(2,128)} %get-tuple-element.29), channel_id=1, source_target_pairs={{1,0},{2,1},{3,2},{4,3},{5,4},{6,5},{7,6},{8,7},{9,8},{10,9},{11,1... | collective-permute-start | bytes 393224 | tf_op jit(solution)/shard_map/ppermute | solution.py:19
  63.1 47.2 %collective-permute-start.5 = (f32[16,128,256]{2,0,1:T(8,128)S(1)}, f32[16,128,256]{2,0,1:T(8,128)S(1)}, u32[]{:S(2)}, u32[]{:S(2)}) collective-permute-start(f32[16,128,256]{2,0,1:T(8,128)S(1)} %broadcast_select_fusion), channel_id=1, source_target_pairs={{0,12},{1,13},{2,14},{3,15},{4,0},{5,1},{6,2},{7,3},{8,4},{9,5},{1... | collective-permute-start | bytes 6291464 | tf_op jit(solution)/shard_map/ppermute | solution.py:28
  110.6 91.6 %collective-permute-start.6 = (f32[16,128,256]{2,0,1:T(8,128)S(1)}, f32[16,128,256]{2,0,1:T(8,128)S(1)}, u32[]{:S(2)}, u32[]{:S(2)}) collective-permute-start(f32[16,128,256]{2,0,1:T(8,128)S(1)} %broadcast_select_fusion.1), channel_id=1, source_target_pairs={{0,8},{1,9},{2,10},{3,11},{4,12},{5,13},{6,14},{7,15},{8,0},{9,1},... | collective-permute-start | bytes 6291464 | tf_op jit(solution)/shard_map/ppermute | solution.py:28
  224.2 9.3 %copy-start.16 = (f32[1,16,32766]{2,1,0:T(8,128)S(1)}, f32[1,16,32766]{2,1,0:T(8,128)}, u32[]{:S(2)}) copy-start(f32[1,16,32766]{2,1,0:T(8,128)} %get-tuple-element.48) | copy-start | bytes 6291076
  226.6 6.8 %copy-start.13 = (f32[1,16,32767]{2,1,0:T(8,128)S(1)}, f32[1,16,32767]{2,1,0:T(8,128)}, u32[]{:S(2)}) copy-start(f32[1,16,32767]{2,1,0:T(8,128)} %get-tuple-element.51) | copy-start | bytes 6291268
  226.6 6.8 %copy-start.14 = (f32[1,16,32767]{2,1,0:T(8,128)S(1)}, f32[1,16,32767]{2,1,0:T(8,128)}, u32[]{:S(2)}) copy-start(f32[1,16,32767]{2,1,0:T(8,128)} %get-tuple-element.52) | copy-start | bytes 6291268
  226.7 6.8 %copy-start.15 = (f32[1,16,32766]{2,1,0:T(8,128)S(1)}, f32[1,16,32766]{2,1,0:T(8,128)}, u32[]{:S(2)}) copy-start(f32[1,16,32766]{2,1,0:T(8,128)} %get-tuple-element.47) | copy-start | bytes 6291076
  229.2 11.2 %collective-permute-start.7 = (f32[1,2,32768]{2,1,0:T(2,128)}, f32[1,2,32768]{2,1,0:T(2,128)}, u32[]{:S(2)}, u32[]{:S(2)}) collective-permute-start(f32[1,2,32768]{2,1,0:T(2,128)} %get-tuple-element.43), channel_id=1, source_target_pairs={{1,0},{2,1},{3,2},{4,3},{5,4},{6,5},{7,6},{8,7},{9,8},{10,9},{11,1... | collective-permute-start | bytes 786440 | tf_op jit(solution)/shard_map/ppermute | solution.py:19
  237.2 8.7 %collective-permute-start.8 = (f32[1,2,32768]{2,1,0:T(2,128)}, f32[1,2,32768]{2,1,0:T(2,128)S(1)}, u32[]{:S(2)}, u32[]{:S(2)}) collective-permute-start(f32[1,2,32768]{2,1,0:T(2,128)} %get-tuple-element.44), channel_id=1, source_target_pairs={{0,1},{1,2},{2,3},{3,4},{4,5},{5,6},{6,7},{7,8},{8,9},{9,10},{10,1... | collective-permute-start | bytes 786440 | tf_op jit(solution)/shard_map/ppermute | solution.py:17
  249.8 7.1 %copy-start = (f32[1,16,32768]{2,1,0:T(8,128)}, f32[1,16,32768]{2,1,0:T(8,128)S(1)}, u32[]{:S(2)}) copy-start(f32[1,16,32768]{2,1,0:T(8,128)S(1)} %fusion.10) | copy-start | bytes 6291460
  267.8 11.5 %copy-start.25 = (f32[1,16,16384]{2,1,0:T(8,128)S(1)}, f32[1,16,16384]{2,1,0:T(8,128)}, u32[]{:S(2)}) copy-start(f32[1,16,16384]{2,1,0:T(8,128)} %get-tuple-element.7) | copy-start | bytes 3145732
  267.8 12.9 %copy-start.11 = (f32[1,16,32766]{2,1,0:T(8,128)S(1)}, f32[1,16,32766]{2,1,0:T(8,128)}, u32[]{:S(2)}) copy-start(f32[1,16,32766]{2,1,0:T(8,128)} %get-tuple-element.37) | copy-start | bytes 6291076
  267.8 12.9 %copy-start.12 = (f32[1,16,32766]{2,1,0:T(8,128)S(1)}, f32[1,16,32766]{2,1,0:T(8,128)}, u32[]{:S(2)}) copy-start(f32[1,16,32766]{2,1,0:T(8,128)} %get-tuple-element.38) | copy-start | bytes 6291076
  267.8 12.9 %copy-start.37 = (f32[1,16,1]{2,1,0:T(8,128)S(1)}, f32[1,16,1]{2,1,0:T(8,128)}, u32[]{:S(2)}) copy-start(f32[1,16,1]{2,1,0:T(8,128)} %get-tuple-element.40) | copy-start | bytes 196
  270.3 18.7 %collective-permute-start.10 = (f32[1,2,32768]{2,1,0:T(2,128)}, f32[1,2,32768]{2,1,0:T(2,128)S(1)}, u32[]{:S(2)}, u32[]{:S(2)}) collective-permute-start(f32[1,2,32768]{2,1,0:T(2,128)} %get-tuple-element.34), channel_id=1, source_target_pairs={{0,1},{1,2},{2,3},{3,4},{4,5},{5,6},{6,7},{7,8},{8,9},{9,10},{10,1... | collective-permute-start | bytes 786440 | tf_op jit(solution)/shard_map/ppermute | solution.py:17
  270.4 18.7 %collective-permute-start.9 = (f32[1,2,32768]{2,1,0:T(2,128)}, f32[1,2,32768]{2,1,0:T(2,128)}, u32[]{:S(2)}, u32[]{:S(2)}) collective-permute-start(f32[1,2,32768]{2,1,0:T(2,128)} %get-tuple-element.33), channel_id=1, source_target_pairs={{1,0},{2,1},{3,2},{4,3},{5,4},{6,5},{7,6},{8,7},{9,8},{10,9},{11,1... | collective-permute-start | bytes 786440 | tf_op jit(solution)/shard_map/ppermute | solution.py:19
  274.8 21.1 %collective-permute-start.3 = (f32[1,2,16384]{2,1,0:T(2,128)}, f32[1,2,16384]{2,1,0:T(2,128)S(1)}, u32[]{:S(2)}, u32[]{:S(2)}) collective-permute-start(f32[1,2,16384]{2,1,0:T(2,128)} %get-tuple-element.94), channel_id=1, source_target_pairs={{0,1},{1,2},{2,3},{3,4},{4,5},{5,6},{6,7},{7,8},{8,9},{9,10},{10,1... | collective-permute-start | bytes 393224 | tf_op jit(solution)/shard_map/ppermute | solution.py:17
  274.8 21.1 %collective-permute-start.2 = (f32[1,2,16384]{2,1,0:T(2,128)}, f32[1,2,16384]{2,1,0:T(2,128)}, u32[]{:S(2)}, u32[]{:S(2)}) collective-permute-start(f32[1,2,16384]{2,1,0:T(2,128)} %get-tuple-element.93), channel_id=1, source_target_pairs={{1,0},{2,1},{3,2},{4,3},{5,4},{6,5},{7,6},{8,7},{9,8},{10,9},{11,1... | collective-permute-start | bytes 393224 | tf_op jit(solution)/shard_map/ppermute | solution.py:19
  296.0 8.7 %copy-start.5 = (f32[16,128,128]{2,1,0:T(8,128)S(1)}, f32[16,128,128]{2,1,0:T(8,128)}, u32[]{:S(2)}) copy-start(f32[16,128,128]{2,1,0:T(8,128)} %slice.408) | copy-start | bytes 3145732
  296.0 12.9 %copy-start.21 = (f32[1,16,16382]{2,1,0:T(8,128)S(1)}, f32[1,16,16382]{2,1,0:T(8,128)}, u32[]{:S(2)}) copy-start(f32[1,16,16382]{2,1,0:T(8,128)} %get-tuple-element.69) | copy-start | bytes 3145348
  296.1 12.9 %copy-start.22 = (f32[1,16,16382]{2,1,0:T(8,128)S(1)}, f32[1,16,16382]{2,1,0:T(8,128)}, u32[]{:S(2)}) copy-start(f32[1,16,16382]{2,1,0:T(8,128)} %get-tuple-element.72) | copy-start | bytes 3145348
  296.1 12.8 %copy-start.23 = (f32[1,16,16383]{2,1,0:T(8,128)S(1)}, f32[1,16,16383]{2,1,0:T(8,128)}, u32[]{:S(2)}) copy-start(f32[1,16,16383]{2,1,0:T(8,128)} %get-tuple-element.61) | copy-start | bytes 3145540
  296.1 12.8 %copy-start.24 = (f32[1,16,16383]{2,1,0:T(8,128)S(1)}, f32[1,16,16383]{2,1,0:T(8,128)}, u32[]{:S(2)}) copy-start(f32[1,16,16383]{2,1,0:T(8,128)} %get-tuple-element.64) | copy-start | bytes 3145540
  296.1 12.8 %copy-start.34 = (f32[1,16,1]{2,1,0:T(8,128)S(1)}, f32[1,16,1]{2,1,0:T(8,128)}, u32[]{:S(2)}) copy-start(f32[1,16,1]{2,1,0:T(8,128)} %get-tuple-element.65) | copy-start | bytes 196
  296.1 12.8 %copy-start.35 = (f32[1,16,1]{2,1,0:T(8,128)S(1)}, f32[1,16,1]{2,1,0:T(8,128)}, u32[]{:S(2)}) copy-start(f32[1,16,1]{2,1,0:T(8,128)} %get-tuple-element.68) | copy-start | bytes 196
  304.8 4.2 %copy-start.6 = (f32[1,16,16384]{2,1,0:T(8,128)S(1)}, f32[1,16,16384]{2,1,0:T(8,128)}, u32[]{:S(2)}) copy-start(f32[1,16,16384]{2,1,0:T(8,128)} %reshape.1144) | copy-start | bytes 3145732
  304.8 4.2 %copy-start.7 = (f32[1,16,16384]{2,1,0:T(8,128)S(1)}, f32[1,16,16384]{2,1,0:T(8,128)}, u32[]{:S(2)}) copy-start(f32[1,16,16384]{2,1,0:T(8,128)} %reshape.1143) | copy-start | bytes 3145732
  (23 other events, 87.0 us)
where the time goes:
time: 315 us; the launch traced here: 314 us
  waiting for transfers between devices  171 us (54%)
  local copies, waits for them, and re-layouts  66.5 us (21%)
  other arithmetic  44.6 us (14%)
  starting transfers between devices  28.4 us (9%)
  between operations  3.98 us (1%)
    ppermute x3, waiting for transfers between devices, passed_along(): return lax.ppermute(x, axis, [(i, (i + by) % size) for i in range(size)])  167 us
    ppermute x4, starting transfers between devices, with_halo(): lax.ppermute(head, axis, [((i + 1) % count, i) for i in range(count)])  17.6 us
    ppermute x3, starting transfers between devices, passed_along(): return lax.ppermute(x, axis, [(i, (i + by) % size) for i in range(size)])  10.8 us
    mul x1, other arithmetic, assemble(): rotation = 0.5 * (total_rc - total_cr)  8.67 us
    slice x6, local copies, waits for them, and re-layouts, column_slope(): jnp.roll(field, -1, 2) - jnp.roll(field, 1, 2)  8.17 us
    slice x6, local copies, waits for them, and re-layouts, column_slope(): jnp.roll(field, -2, 2) - jnp.roll(field, 2, 2)  7.96 us
    reshape x3, local copies, waits for them, and re-layouts, per_device(): member[0].reshape(height, blocks, 256)[:, :, 64:192]  7.29 us
    slice x6, local copies, waits for them, and re-layouts, column_slope(): jnp.roll(field, 1, 2)  6.93 us
  transfers between devices with their start and end apart: 11, of which 4 were waited for; matrix products, arithmetic and copies ran while one was open for 23% of the time, Pallas kernels for 0%

commit v1 on v0

v1 whole, which is shorter than its diff:
```python
import functools

import jax
import jax.numpy as jnp
from jax import lax
from jax.experimental import pallas as pl
from jax.experimental.pallas import tpu as pltpu
from jax.sharding import PartitionSpec as P

RB = 8
BITS = 3
LANES = 128
HALO = 4
PER_EDGE = LANES // (2 * HALO)
SPARE = 12
TILE = 16


def passed_along(x, axis, by):
    size = lax.axis_size(axis)
    return lax.ppermute(x, axis, [(i, (i + by) % size) for i in range(size)])


def edge_of(left, right, lane):
    return jnp.where(lane < LANES // 2, right, left)


def pack_kernel(cap, blocks, src_ref, pot_ref, out_ref):
    group = pl.program_id(0)
    rows = pot_ref.shape[1]
    lane = lax.broadcasted_iota(jnp.int32, (rows, LANES), 1)

    def at(s):
        return pot_ref[0, :, pl.ds(pl.multiple_of(s * LANES, LANES), LANES)]

    packed = None
    for j in range(cap):
        s = src_ref[group * cap + j]
        left = at(jnp.where(s == 0, blocks - 1, s - 1))
        right = at(jnp.where(s == blocks - 1, 0, s + 1))
        out_ref[0, j] = at(s)
        spot = j % PER_EDGE
        edge = pltpu.roll(edge_of(left, right, lane), HALO + 2 * HALO * spot, 1)
        packed = edge if spot == 0 else jnp.where(lane >= 2 * HALO * spot, edge, packed)
        if spot == PER_EDGE - 1 or j == cap - 1:
            out_ref[0, cap + j // PER_EDGE] = packed


def exchange_kernel(stride, devices, buf_ref, out_ref, send_sem, recv_sem, own_sem):
    me = lax.axis_index("row")
    barrier = pltpu.get_barrier_semaphore()
    for k in range(1, RB):
        pl.semaphore_signal(
            barrier,
            inc=1,
            device_id={"row": lax.rem(me + stride * k, devices)},
            device_id_type=pl.DeviceIdType.MESH,
        )
    pl.semaphore_wait(barrier, RB - 1)
    copies = []
    for k in range(1, RB):
        copy = pltpu.make_async_remote_copy(
            src_ref=buf_ref.at[k],
            dst_ref=out_ref.at[k],
            send_sem=send_sem.at[k],
            recv_sem=recv_sem.at[k],
            device_id={"row": lax.rem(me + devices - stride * k, devices)},
            device_id_type=pl.DeviceIdType.MESH,
        )
        copy.start()
        copies.append(copy)
    own = pltpu.make_async_copy(buf_ref.at[0], out_ref.at[0], own_sem)
    own.start()
    own.wait()
    for copy in copies:
        copy.wait()


def shifted(middle, edge, lane, by):
    if by > 0:
        return pltpu.roll(jnp.where(lane < by, edge, middle), LANES - by, 1)
    return pltpu.roll(jnp.where(lane >= LANES + by, edge, middle), -by, 1)


def second(x, total):
    return (
        (x[4] + x[-4]) - 16.0 * (x[3] + x[-3]) + 64.0 * (x[2] + x[-2])
        + 16.0 * (x[1] + x[-1]) - 130.0 * total
    ) * (1.0 / 144.0)


def first(x):
    return (8.0 * (x[1] - x[-1]) - (x[2] - x[-2])) * (1.0 / 12.0)


def fields(middle, edge, height):
    lane = lax.broadcasted_iota(jnp.int32, (height, LANES), 1)
    near = [o for o in range(-HALO, HALO + 1) if o]
    centre = middle(0)
    side = edge(0)
    along_rows = {o: middle(o) for o in near}
    slope_r = first(along_rows)
    slope_r_side = first({o: edge(o) for o in (-2, -1, 1, 2)})
    along_cols = {o: shifted(centre, side, lane, o) for o in near}
    slope_c = first(along_cols)
    curve_rc = first({o: shifted(slope_r, slope_r_side, lane, o) for o in (-2, -1, 1, 2)})
    return slope_r, slope_c, second(along_rows, centre), curve_rc, second(along_cols, centre)


def compute_kernel(blocks, where_ref, ratio_ref, pot_ref, win_ref, conv_ref, shear_ref, rot_ref, disp_ref, edges):
    height = conv_ref.shape[0]
    rows = pot_ref.shape[1]
    step = pl.program_id(0)
    beta_near, beta_one, beta_two = ratio_ref[0], ratio_ref[1], ratio_ref[2]
    lane = lax.broadcasted_iota(jnp.int32, (rows, LANES), 1)

    def body(t, carry):
        b = step * TILE + t

        def columns(s):
            return pl.ds(pl.multiple_of(s * LANES, LANES), LANES)

        here = columns(b)
        left = pot_ref[0, :, columns(jnp.where(b == 0, blocks - 1, b - 1))]
        right = pot_ref[0, :, columns(jnp.where(b == blocks - 1, 0, b + 1))]
        edges[0] = edge_of(left, right, lane)
        window = where_ref[b]
        edges[1] = pltpu.roll(win_ref[where_ref[blocks + b]], where_ref[2 * blocks + b], 1)
        near_r, near_c, near_rr, near_rc, near_cc = fields(
            lambda o: pot_ref[0, HALO + o : HALO + o + height, here],
            lambda o: edges[0, HALO + o : HALO + o + height],
            height,
        )
        far_r, far_c, far_rr, far_rc, far_cc = fields(
            lambda o: win_ref[window, HALO + o : HALO + o + height],
            lambda o: edges[1, HALO + o : HALO + o + height],
            height,
        )
        inner_rr = 1.0 - beta_near * near_rr
        inner_rc = -beta_near * near_rc
        inner_cc = 1.0 - beta_near * near_cc
        chain_rr = far_rr * inner_rr + far_rc * inner_rc
        chain_rc = far_rr * inner_rc + far_rc * inner_cc
        chain_cr = far_rc * inner_rr + far_cc * inner_rc
        chain_cc = far_rc * inner_rc + far_cc * inner_cc
        total_rr = 1.0 - beta_one * near_rr - beta_two * chain_rr
        total_rc = -beta_one * near_rc - beta_two * chain_rc
        total_cr = -beta_one * near_rc - beta_two * chain_cr
        total_cc = 1.0 - beta_one * near_cc - beta_two * chain_cc
        there = columns(t)
        conv_ref[:, there] = 1.0 - 0.5 * (total_rr + total_cc)
        shear_ref[0, :, there] = 0.5 * (total_rr - total_cc)
        shear_ref[1, :, there] = -0.5 * (total_rc + total_cr)
        rot_ref[:, there] = 0.5 * (total_rc - total_cr)
        disp_ref[0, :, there] = beta_one * near_r + beta_two * far_r
        disp_ref[1, :, there] = beta_one * near_c + beta_two * far_c
        return carry

    lax.fori_loop(0, TILE, body, 0, unroll=2)


def per_device(potentials, ratios, row_offset, col_offset):
    devices = lax.axis_size("row")
    height, columns = potentials.shape[1:]
    blocks = columns // LANES
    stride = devices // RB
    cap = min(blocks, blocks // RB + SPARE)
    edge_windows = -(-cap // PER_EDGE)
    group = cap + edge_windows
    rows = height + 2 * HALO
    every = jnp.arange(blocks, dtype=jnp.int32)

    counts = jnp.sum(row_offset[:, None] == jnp.arange(RB, dtype=jnp.int32)[None, :], axis=0)
    fullest = jnp.max(counts)
    other = row_offset
    for _ in range(1, lax.axis_size("cosmo")):
        other = passed_along(other, "cosmo", 1)
        theirs = jnp.sum(other[:, None] == jnp.arange(RB, dtype=jnp.int32)[None, :], axis=0)
        fullest = jnp.maximum(fullest, jnp.max(theirs))
    fits = fullest <= cap

    rank = jnp.sum((row_offset[:, None] == row_offset[None, :]) & (every[None, :] < every[:, None]), axis=1)
    slot = jnp.where(fits, row_offset * cap + rank.astype(jnp.int32), every)
    source = (every + col_offset) % blocks
    is_slot = slot[None, :] == jnp.arange(RB * cap, dtype=jnp.int32)[:, None]
    sources = jnp.sum(jnp.where(is_slot, source[None, :], 0), axis=1).astype(jnp.int32)
    chunk, spot = slot // cap, slot % cap
    where = jnp.concatenate([
        chunk * group + spot,
        chunk * group + cap + spot // PER_EDGE,
        LANES - HALO - 2 * HALO * (spot % PER_EDGE),
    ]).astype(jnp.int32)

    above = passed_along(potentials[:, height - HALO :], "row", 1)
    below = passed_along(potentials[:, :HALO], "row", devices - 1)
    padded = jnp.concatenate([above, potentials, below], axis=1)

    packed = pl.pallas_call(
        functools.partial(pack_kernel, cap, blocks),
        out_shape=jax.ShapeDtypeStruct((RB, group, rows, LANES), jnp.float32),
        grid_spec=pltpu.PrefetchScalarGridSpec(
            num_scalar_prefetch=1,
            grid=(RB,),
            in_specs=[pl.BlockSpec((1, rows, columns), lambda g, _: (1, 0, 0))],
            out_specs=pl.BlockSpec((1, group, rows, LANES), lambda g, _: (g, 0, 0, 0)),
        ),
    )(sources, padded)

    def direct(packed):
        return pl.pallas_call(
            functools.partial(exchange_kernel, stride, devices),
            out_shape=jax.ShapeDtypeStruct(packed.shape, packed.dtype),
            in_specs=[pl.BlockSpec(memory_space=pltpu.VMEM)],
            out_specs=pl.BlockSpec(memory_space=pltpu.VMEM),
            scratch_shapes=[
                pltpu.SemaphoreType.DMA((RB,)),
                pltpu.SemaphoreType.DMA((RB,)),
                pltpu.SemaphoreType.DMA,
            ],
            compiler_params=pltpu.CompilerParams(collective_id=0, has_side_effects=True),
        )(packed)

    def by_bits(packed):
        offsets = jnp.sum(jnp.where(is_slot, row_offset[None, :], 0), axis=1).astype(jnp.int32).reshape(RB, cap)
        of_edges = jnp.pad(offsets, ((0, 0), (0, edge_windows * PER_EDGE - cap)))
        of_edges = jnp.repeat(of_edges.reshape(RB, edge_windows, PER_EDGE), 2 * HALO, axis=2)
        lanes = jnp.concatenate([jnp.broadcast_to(offsets[:, :, None], (RB, cap, LANES)), of_edges], axis=1)
        for bit in range(BITS):
            arrived = passed_along(packed, "row", devices - stride * 2**bit)
            picked = lanes // 2**bit % 2 == 1
            packed = jnp.where(picked[:, :, None, :], arrived, packed)
        return packed

    windows = lax.cond(fits, direct, by_bits, packed).reshape(RB * group, rows, LANES)

    wide = TILE * LANES
    return pl.pallas_call(
        functools.partial(compute_kernel, blocks),
        out_shape=(
            jax.ShapeDtypeStruct((height, columns), jnp.float32),
            jax.ShapeDtypeStruct((2, height, columns), jnp.float32),
            jax.ShapeDtypeStruct((height, columns), jnp.float32),
            jax.ShapeDtypeStruct((2, height, columns), jnp.float32),
        ),
        grid_spec=pltpu.PrefetchScalarGridSpec(
            num_scalar_prefetch=2,
            grid=(blocks // TILE,),
            in_specs=[
                pl.BlockSpec((1, rows, columns), lambda g, *_: (0, 0, 0)),
                pl.BlockSpec((RB * group, rows, LANES), lambda g, *_: (0, 0, 0)),
            ],
            out_specs=(
                pl.BlockSpec((height, wide), lambda g, *_: (0, g)),
                pl.BlockSpec((2, height, wide), lambda g, *_: (0, 0, g)),
                pl.BlockSpec((height, wide), lambda g, *_: (0, g)),
                pl.BlockSpec((2, height, wide), lambda g, *_: (0, 0, g)),
            ),
            scratch_shapes=[pltpu.VMEM((2, rows, LANES), jnp.float32)],
        ),
    )(where, ratios, padded, windows)


def solution(mesh):
    return jax.shard_map(
        per_device,
        mesh=mesh,
        in_specs=(P("cosmo", "row", None), P("cosmo"), P("cosmo"), P("cosmo")),
        out_specs=(
            P(("cosmo", "row"), None),
            P(None, ("cosmo", "row"), None),
            P(("cosmo", "row"), None),
            P(None, ("cosmo", "row"), None),
        ),
        check_vma=False,
    )
```

time: 315 us -> 117 us (0.37)
  waiting for transfers between devices: 171 us -> 0.16 us
  Pallas kernels: 0 us -> 96.4 us
  local copies, waits for them, and re-layouts: 66.5 us -> 2.69 us
  other arithmetic: 44.6 us -> 7.77 us
  starting transfers between devices: 28.4 us -> 7.47 us
    ppermute x3, waiting for transfers between devices: 167 us -> 0.16 us  [passed_along(): return lax.ppermute(x, axis, [(i, (i + by) % size) for i in range(size)])]
    pallas_call x0 -> x3, Pallas kernels: none -> 96.4 us  [the longest x1 74.2 us: direct(): pl.pallas_call(functools.partial(exchange_kernel, stride, devices), out_s...]
    slice x34 -> x1, local copies, waits for them, and re-layouts: 40.3 us -> 2.69 us  [per_device(): above = passed_along(potentials[:, height - HALO:], 'row', 1)]
    ppermute x8 -> x0, starting transfers between devices: 17.6 us -> none  [the longest x4 17.6 us: with_halo(): lax.ppermute(head, axis, [((i + 1) % count, i) for i in range(count)])]
    mul x5 -> x0, other arithmetic: 15.3 us -> none  [the longest x1 8.67 us: assemble(): rotation = 0.5 * (total_rc - total_cr)]
    div x7 -> x0, other arithmetic: 9.95 us -> none  [the longest x3 6.4 us: row_slope(): (8.0 * (padded[:, 3:height + 3] - padded[:, 1:height + 1]) - (padded[:, 4...]
    reshape x4 -> x0, local copies, waits for them, and re-layouts: 9.04 us -> none  [the longest x3 7.29 us: per_device(): member[0].reshape(height, blocks, 256)[:, :, 64:192]]
    add x2, other arithmetic: 7.54 us -> 0.69 us  [the longest x1 0.68 us: per_device(): chunk * group + spot]
  transfers between devices with their start and end apart: 11 -> 3, of which waited for: 4 -> 1; matrix products, arithmetic and copies ran while one was open for 23% -> 7% of each run, Pallas kernels for 0% -> 0%
where the time goes in v1:
time: 117 us
  Pallas kernels  96.4 us (82%)
  other arithmetic  7.77 us (7%)
  starting transfers between devices  7.47 us (6%)
  local copies, waits for them, and re-layouts  2.69 us (2%)
  between operations  1.99 us (2%)
    pallas_call x1, Pallas kernels, direct(): pl.pallas_call(functools.partial(exchange_kernel, stride, devices), out_s...  74.2 us
    pallas_call x1, Pallas kernels, per_device(): pl.pallas_call(functools.partial(compute_kernel, blocks), out_shape=(jax....  18.1 us
    ppermute x3, starting transfers between devices, passed_along(): return lax.ppermute(x, axis, [(i, (i + by) % size) for i in range(size)])  7.47 us
    pallas_call x1, Pallas kernels, per_device(): pl.pallas_call(functools.partial(pack_kernel, cap, blocks), out_shape=jax...  4.14 us
    slice x1, local copies, waits for them, and re-layouts, per_device(): above = passed_along(potentials[:, height - HALO:], 'row', 1)  2.69 us
  transfers between devices with their start and end apart: 3, of which 1 were waited for; matrix products, arithmetic and copies ran while one was open for 7% of the time, Pallas kernels for 0%

profile of v1, /device:TPU:0, one launch (start us, length us, event | category | flops | bytes accessed | tf_op | source)
XLA Modules:
  0.0 116.5 jit_solution(15695190951281527221)
XLA Ops:
  0.6 0.0 copy-start
  0.6 3.0 %collective-permute-start.3 = (s32[128]{0:T(128)}, s32[128]{0:T(128)S(1)}, u32[]{:S(2)}, u32[]{:S(2)}) collective-permute-start(s32[128]{0:T(128)} %param.8), channel_id=1, source_target_pairs={{0,16},{16,0},{1,17},{17,1},{2,18},{18,2},{3,19},{19,3},{4,20},{20... | collective-permute-start | bytes 1544 | tf_op jit(solution)/shard_map/ppermute | solution.py:21
  3.7 2.7 %fusion.22 = (f32[2,4,16384]{2,1,0:T(4,128)}, f32[2,4,16384]{2,1,0:T(4,128)}) fusion(f32[2,16,16384]{2,1,0:T(8,128)} %param.6), kind=kLoop, calls=%fused_computation.62 | loop fusion | bytes 2097152 | tf_op jit(solution)/shard_map/slice | solution.py:194
  6.4 0.0 collective-permute-start.4
  6.4 4.4 %collective-permute-start.5 = (f32[2,4,16384]{2,1,0:T(4,128)}, f32[2,4,16384]{2,1,0:T(4,128)S(1)}, u32[]{:S(2)}, u32[]{:S(2)}) collective-permute-start(f32[2,4,16384]{2,1,0:T(4,128)} %get-tuple-element.26), channel_id=1, source_target_pairs={{0,15},{1,0},{2,1},{3,2},{4,3},{5,4},{6,5},{7,6},{8,7},{9,8},{10,9... | collective-permute-start | bytes 1572872 | tf_op jit(solution)/shard_map/ppermute | solution.py:21
  10.8 0.9 convert_reduce_fusion
  11.7 0.7 and_select_fusion
  12.4 0.8 convert_reduce_fusion.2
  13.1 0.6 reduce_max.18
  13.8 0.0 collective-permute-done.3
  13.8 0.1 convert_reduce_fusion.1
  13.9 0.6 reduce_max.19
  15.8 0.7 fusion.20
  16.5 0.6 pad_add_fusion.1.where_ref
  17.1 0.7 select_reduce_fusion.1.src_ref
  17.8 0.2 collective-permute-done.4
  18.0 0.0 collective-permute-done.5
  18.0 0.0 copy-done
  18.0 2.1 %pad_maximum_fusion.pot_ref = f32[2,24,16384]{2,1,0:T(8,128)} fusion(f32[2,4,16384]{2,1,0:T(4,128)S(1)} %collective-permute-done.5, f32[2,16,16384]{2,1,0:T(8,128)S(1)} %copy-done, f32[2,4,16384]{2,1,0:T(4,128)S(1)} %collective-permute-done.4), kind=kLoop, calls=%fused_computation.34 | loop fusion | flops 1572864 | bytes 6291456 | tf_op jit(solution)/shard_map/concatenate | solution.py:196
  20.1 0.0 copy-start.1
  20.1 4.1 %shard_map.75 = f32[8,30,24,128]{3,2,1,0:T(8,128)S(1)} custom-call(s32[224]{0:T(256)} %select_reduce_fusion.1.src_ref, f32[2,24,16384]{2,1,0:T(8,128)} %pad_maximum_fusion.pot_ref), custom_call_target="tpu_custom_call" | custom-call | tf_op jit(solution)/shard_map/pallas_call | solution.py:198
  24.2 0.0 copy-done.1
  24.2 74.3 %conditional.1 = (f32[240,24,128]{2,1,0:T(8,128)}) conditional(s32[]{:T(128)} %convert_element_type.15, (s32[128]{0:T(128)S(1)}, pred[224,128]{1,0:T(8,128)(4,1)S(1)}, f32[8,30,24,128]{3,2,1,0:T(8,128)S(1)}) %tuple.25, f32[8,30,24,128]{3,2,1,0:T(8,128)S(1)} %shard_map.75), branch_computations={%region_6.8_spmd, %region_8.9_spmd} | conditional | flops 3958560 | bytes 62434308 | solution.py:234
  24.2 74.2 %branch_1_fun.1 = f32[8,30,24,128]{3,2,1,0:T(8,128)} custom-call(f32[8,30,24,128]{3,2,1,0:T(8,128)S(1)} %buf_ref), custom_call_target="tpu_custom_call" | custom-call | tf_op jit(solution)/shard_map/cond/branch_1_fun/pallas_call | solution.py:210
  98.5 18.1 %shard_map.76 = (f32[16,16384]{1,0:T(8,128)}, f32[2,16,16384]{2,1,0:T(8,128)}, f32[16,16384]{1,0:T(8,128)}, f32[2,16,16384]{2,1,0:T(8,128)}) custom-call(s32[384]{0:T(512)} %pad_add_fusion.1.where_ref, f32[3]{0:T(128)} %ratio_ref.1, f32[2,24,16384]{2,1,0:T(8,128)} %pad_maximum_fusion.pot_ref, f32[240,24,128]{2,1,0:T(8,128)} %get-tuple-element.29.win_ref), custom_call_target="tpu_custom_call" | custom-call | tf_op jit(solution)/shard_map/pallas_call | solution.py:237
  (2 shorter events, 0.0 us)
Async XLA Ops:
  0.6 17.3 %copy-start = (f32[2,16,16384]{2,1,0:T(8,128)S(1)}, f32[2,16,16384]{2,1,0:T(8,128)}, u32[]{:S(2)}) copy-start(f32[2,16,16384]{2,1,0:T(8,128)} %param.6) | copy-start | bytes 6291460
  0.6 13.1 %collective-permute-start.3 = (s32[128]{0:T(128)}, s32[128]{0:T(128)S(1)}, u32[]{:S(2)}, u32[]{:S(2)}) collective-permute-start(s32[128]{0:T(128)} %param.8), channel_id=1, source_target_pairs={{0,16},{16,0},{1,17},{17,1},{2,18},{18,2},{3,19},{19,3},{4,20},{20... | collective-permute-start | bytes 1544 | tf_op jit(solution)/shard_map/ppermute | solution.py:21
  6.4 11.6 %collective-permute-start.4 = (f32[2,4,16384]{2,1,0:T(4,128)}, f32[2,4,16384]{2,1,0:T(4,128)S(1)}, u32[]{:S(2)}, u32[]{:S(2)}) collective-permute-start(f32[2,4,16384]{2,1,0:T(4,128)} %get-tuple-element.25), channel_id=1, source_target_pairs={{0,1},{1,2},{2,3},{3,4},{4,5},{5,6},{6,7},{7,8},{8,9},{9,10},{10,1... | collective-permute-start | bytes 1572872 | tf_op jit(solution)/shard_map/ppermute | solution.py:21
  6.4 11.6 %collective-permute-start.5 = (f32[2,4,16384]{2,1,0:T(4,128)}, f32[2,4,16384]{2,1,0:T(4,128)S(1)}, u32[]{:S(2)}, u32[]{:S(2)}) collective-permute-start(f32[2,4,16384]{2,1,0:T(4,128)} %get-tuple-element.26), channel_id=1, source_target_pairs={{0,15},{1,0},{2,1},{3,2},{4,3},{5,4},{6,5},{7,6},{8,7},{9,8},{10,9... | collective-permute-start | bytes 1572872 | tf_op jit(solution)/shard_map/ppermute | solution.py:21
  20.1 4.2 %copy-start.1 = (s32[128]{0:T(128)S(1)}, s32[128]{0:T(128)}, u32[]{:S(2)}) copy-start(s32[128]{0:T(128)} %param.8) | copy-start | bytes 1540

commit v2 on v1

v2 whole, which is shorter than its diff:
```python
import functools

import jax
import jax.numpy as jnp
from jax import lax
from jax.experimental import pallas as pl
from jax.experimental.pallas import tpu as pltpu
from jax.sharding import PartitionSpec as P

RB = 8
BITS = 3
LANES = 128
HALO = 4
PER_EDGE = LANES // (2 * HALO)
SPARES = (6, 8, 10, 12, 16)
TILE = 16


def passed_along(x, axis, by):
    size = lax.axis_size(axis)
    return lax.ppermute(x, axis, [(i, (i + by) % size) for i in range(size)])


def edge_of(left, right, lane):
    return jnp.where(lane < LANES // 2, right, left)


def pack_kernel(cap, edge_windows, blocks, src_ref, pot_ref, out_ref):
    group = pl.program_id(0)
    rows = pot_ref.shape[1]
    lane = lax.broadcasted_iota(jnp.int32, (rows, LANES), 1)

    def columns(s):
        return pl.ds(pl.multiple_of(s * LANES, LANES), LANES)

    packed = None
    for j in range(cap):
        s = src_ref[group * cap + j]
        left = pot_ref[0, :, columns(jnp.where(s == 0, blocks - 1, s - 1))]
        right = pot_ref[0, :, columns(jnp.where(s == blocks - 1, 0, s + 1))]
        for q in range(rows // HALO):
            out_ref[0, q, edge_windows + j] = pot_ref[0, HALO * q : HALO * (q + 1), columns(s)]
        spot = j % PER_EDGE
        edge = pltpu.roll(edge_of(left, right, lane), HALO + 2 * HALO * spot, 1)
        packed = edge if spot == 0 else jnp.where(lane >= 2 * HALO * spot, edge, packed)
        if spot == PER_EDGE - 1 or j == cap - 1:
            for q in range(rows // HALO):
                out_ref[0, q, j // PER_EDGE] = packed[HALO * q : HALO * (q + 1)]


def exchange_kernel(
    stride, devices, used, buf_ref, top_ref, bottom_ref, out_ref, above_ref, below_ref,
    send_sem, recv_sem, up_send, up_recv, down_send, down_recv, own_sem,
):
    me = lax.axis_index("row")
    quads = buf_ref.shape[1]
    part = pl.ds(0, used)
    after, before = lax.rem(me + 1, devices), lax.rem(me + devices - 1, devices)
    peers = [lax.rem(me + stride * k, devices) for k in range(1, RB)] + [after, before]
    barrier = pltpu.get_barrier_semaphore()
    for peer in peers:
        pl.semaphore_signal(barrier, inc=1, device_id={"row": peer}, device_id_type=pl.DeviceIdType.MESH)
    pl.semaphore_wait(barrier, len(peers))

    def sent(src, dst, send, recv, to):
        copy = pltpu.make_async_remote_copy(
            src_ref=src, dst_ref=dst, send_sem=send, recv_sem=recv,
            device_id={"row": to}, device_id_type=pl.DeviceIdType.MESH,
        )
        copy.start()
        return copy

    order = sorted(range(1, RB), key=lambda k: abs(k - RB // 2))
    copies = {
        k: sent(
            buf_ref.at[k, :, part], out_ref.at[k, pl.ds(1, quads), part], send_sem.at[k], recv_sem.at[k],
            lax.rem(me + devices - stride * k, devices),
        )
        for k in order
    }
    own = pltpu.make_async_copy(buf_ref.at[0, :, part], out_ref.at[0, pl.ds(1, quads), part], own_sem)
    own.start()
    rims = [
        sent(bottom_ref, above_ref, up_send.at[RB], up_recv.at[RB], after),
        sent(top_ref, below_ref, down_send.at[RB], down_recv.at[RB], before),
        sent(buf_ref.at[0, quads - 1, part], out_ref.at[0, 0, part], up_send.at[0], up_recv.at[0], after),
        sent(buf_ref.at[0, 0, part], out_ref.at[0, quads + 1, part], down_send.at[0], down_recv.at[0], before),
    ]
    for k in order:
        copies[k].wait_recv()
        rims.append(sent(out_ref.at[k, quads, part], out_ref.at[k, 0, part], up_send.at[k], up_recv.at[k], after))
        rims.append(sent(out_ref.at[k, 1, part], out_ref.at[k, quads + 1, part], down_send.at[k], down_recv.at[k], before))
    own.wait()
    for k in order:
        copies[k].wait_send()
    for copy in rims:
        copy.wait()


def shifted(middle, edge, lane, by):
    if by > 0:
        return pltpu.roll(jnp.where(lane < by, edge, middle), LANES - by, 1)
    return pltpu.roll(jnp.where(lane >= LANES + by, edge, middle), -by, 1)


def second(x, total):
    return (
        (x[4] + x[-4]) - 16.0 * (x[3] + x[-3]) + 64.0 * (x[2] + x[-2])
        + 16.0 * (x[1] + x[-1]) - 130.0 * total
    ) * (1.0 / 144.0)


def first(x):
    return (8.0 * (x[1] - x[-1]) - (x[2] - x[-2])) * (1.0 / 12.0)


def fields(middle, edge, height):
    lane = lax.broadcasted_iota(jnp.int32, (height, LANES), 1)
    near = [o for o in range(-HALO, HALO + 1) if o]
    centre = middle(0)
    side = edge(0)
    along_rows = {o: middle(o) for o in near}
    slope_r = first(along_rows)
    slope_r_side = first({o: edge(o) for o in (-2, -1, 1, 2)})
    along_cols = {o: shifted(centre, side, lane, o) for o in near}
    slope_c = first(along_cols)
    curve_rc = first({o: shifted(slope_r, slope_r_side, lane, o) for o in (-2, -1, 1, 2)})
    return slope_r, slope_c, second(along_rows, centre), curve_rc, second(along_cols, centre)


def compute_kernel(
    blocks, where_ref, ratio_ref, pot_ref, above_ref, below_ref, win_ref,
    conv_ref, shear_ref, rot_ref, disp_ref, views,
):
    height = conv_ref.shape[0]
    rows = height + 2 * HALO
    step = pl.program_id(0)
    beta_near, beta_one, beta_two = ratio_ref[0], ratio_ref[1], ratio_ref[2]

    def body(t, carry):
        b = step * TILE + t

        def columns(s):
            return pl.ds(pl.multiple_of(s * LANES, LANES), LANES)

        here = columns(b)
        left = columns(jnp.where(b == 0, blocks - 1, b - 1))
        right = columns(jnp.where(b == blocks - 1, 0, b + 1))
        view = views.at[lax.rem(t, 2)]
        for rim, ref in ((slice(0, HALO), above_ref), (slice(HALO, HALO + height), pot_ref.at[0]), (slice(HALO + height, rows), below_ref)):
            lane = lax.broadcasted_iota(jnp.int32, (ref.shape[0], LANES), 1)
            view[0, rim] = ref[:, here]
            view[1, rim] = edge_of(ref[:, left], ref[:, right], lane)
        chunk, window, edge = where_ref[b], where_ref[blocks + b], where_ref[2 * blocks + b]
        turn = where_ref[3 * blocks + b]
        for q in range(rows // HALO):
            view[2, HALO * q : HALO * (q + 1)] = win_ref[chunk, q, window]
            view[3, HALO * q : HALO * (q + 1)] = win_ref[chunk, q, edge]
        view[3] = pltpu.roll(view[3], turn, 1)

        def rows_of(n):
            return lambda o: view[n, HALO + o : HALO + o + height]

        near_r, near_c, near_rr, near_rc, near_cc = fields(rows_of(0), rows_of(1), height)
        far_r, far_c, far_rr, far_rc, far_cc = fields(rows_of(2), rows_of(3), height)
        inner_rr = 1.0 - beta_near * near_rr
        inner_rc = -beta_near * near_rc
        inner_cc = 1.0 - beta_near * near_cc
        chain_rr = far_rr * inner_rr + far_rc * inner_rc
        chain_rc = far_rr * inner_rc + far_rc * inner_cc
        chain_cr = far_rc * inner_rr + far_cc * inner_rc
        chain_cc = far_rc * inner_rc + far_cc * inner_cc
        total_rr = 1.0 - beta_one * near_rr - beta_two * chain_rr
        total_rc = -beta_one * near_rc - beta_two * chain_rc
        total_cr = -beta_one * near_rc - beta_two * chain_cr
        total_cc = 1.0 - beta_one * near_cc - beta_two * chain_cc
        there = columns(t)
        conv_ref[:, there] = 1.0 - 0.5 * (total_rr + total_cc)
        shear_ref[0, :, there] = 0.5 * (total_rr - total_cc)
        shear_ref[1, :, there] = -0.5 * (total_rc + total_cr)
        rot_ref[:, there] = 0.5 * (total_rc - total_cr)
        disp_ref[0, :, there] = beta_one * near_r + beta_two * far_r
        disp_ref[1, :, there] = beta_one * near_c + beta_two * far_c
        return carry

    lax.fori_loop(0, TILE, body, 0, unroll=2)


def per_device(potentials, ratios, row_offset, col_offset):
    devices = lax.axis_size("row")
    height, columns = potentials.shape[1:]
    blocks = columns // LANES
    stride = devices // RB
    caps = [min(blocks, blocks // RB + spare) for spare in SPARES]
    cap = caps[-1]
    edge_windows = -(-cap // PER_EDGE)
    group = cap + edge_windows
    quads = height // HALO
    every = jnp.arange(blocks, dtype=jnp.int32)

    rank = None
    fullest = 0
    other = row_offset
    for turn in range(lax.axis_size("cosmo")):
        if turn:
            other = passed_along(other, "cosmo", 1)
        ranks = jnp.sum((other[:, None] == other[None, :]) & (every[None, :] < every[:, None]), axis=1, dtype=jnp.int32)
        fullest = jnp.maximum(fullest, jnp.max(ranks) + 1)
        rank = ranks if rank is None else rank
    level = sum((fullest > c).astype(jnp.int32) for c in caps)

    slot = jnp.where(fullest <= cap, row_offset * cap + rank, every)
    source = (every + col_offset) % blocks
    is_slot = slot[None, :] == jnp.arange(RB * cap, dtype=jnp.int32)[:, None]
    sources = jnp.sum(jnp.where(is_slot, source[None, :], 0), axis=1, dtype=jnp.int32)
    spot = slot % cap
    where = jnp.concatenate([
        slot // cap,
        edge_windows + spot,
        spot // PER_EDGE,
        LANES - HALO - 2 * HALO * (spot % PER_EDGE),
    ]).astype(jnp.int32)

    packed = pl.pallas_call(
        functools.partial(pack_kernel, cap, edge_windows, blocks),
        out_shape=jax.ShapeDtypeStruct((RB, quads, group, HALO, LANES), jnp.float32),
        grid_spec=pltpu.PrefetchScalarGridSpec(
            num_scalar_prefetch=1,
            grid=(RB,),
            in_specs=[pl.BlockSpec((1, height, columns), lambda g, _: (1, 0, 0))],
            out_specs=pl.BlockSpec((1, quads, group, HALO, LANES), lambda g, _: (g, 0, 0, 0, 0)),
        ),
    )(sources, potentials)
    top, bottom = potentials[0, :HALO], potentials[0, height - HALO :]
    out_shape = (RB, quads + 2, group, HALO, LANES)

    def direct(n, packed, top, bottom):
        vmem = pl.BlockSpec(memory_space=pltpu.VMEM)
        return pl.pallas_call(
            functools.partial(exchange_kernel, stride, devices, edge_windows + caps[n]),
            out_shape=tuple(jax.ShapeDtypeStruct(x, jnp.float32) for x in (out_shape, top.shape, top.shape)),
            in_specs=[vmem] * 3,
            out_specs=(vmem,) * 3,
            scratch_shapes=[pltpu.SemaphoreType.DMA((RB,))] * 2
            + [pltpu.SemaphoreType.DMA((RB + 1,))] * 4
            + [pltpu.SemaphoreType.DMA],
            compiler_params=pltpu.CompilerParams(collective_id=n, has_side_effects=True),
        )(packed, top, bottom)

    def by_bits(packed, top, bottom):
        offsets = jnp.sum(jnp.where(is_slot, row_offset[None, :], 0), axis=1, dtype=jnp.int32).reshape(RB, cap)
        of_edges = jnp.pad(offsets, ((0, 0), (0, edge_windows * PER_EDGE - cap)))
        of_edges = jnp.repeat(of_edges.reshape(RB, edge_windows, PER_EDGE), 2 * HALO, axis=2)
        lanes = jnp.concatenate([of_edges, jnp.broadcast_to(offsets[:, :, None], (RB, cap, LANES))], axis=1)
        for bit in range(BITS):
            arrived = passed_along(packed, "row", devices - stride * 2**bit)
            picked = lanes // 2**bit % 2 == 1
            packed = jnp.where(picked[:, None, :, None, :], arrived, packed)
        over = passed_along(packed[:, quads - 1 :], "row", 1)
        under = passed_along(packed[:, :1], "row", devices - 1)
        return (
            jnp.concatenate([over, packed, under], axis=1),
            passed_along(bottom, "row", 1),
            passed_along(top, "row", devices - 1),
        )

    branches = [functools.partial(direct, n) for n in range(len(caps))] + [by_bits]
    windows, above, below = lax.switch(level, branches, packed, top, bottom)

    wide = TILE * LANES
    return pl.pallas_call(
        functools.partial(compute_kernel, blocks),
        out_shape=(
            jax.ShapeDtypeStruct((height, columns), jnp.float32),
            jax.ShapeDtypeStruct((2, height, columns), jnp.float32),
            jax.ShapeDtypeStruct((height, columns), jnp.float32),
            jax.ShapeDtypeStruct((2, height, columns), jnp.float32),
        ),
        grid_spec=pltpu.PrefetchScalarGridSpec(
            num_scalar_prefetch=2,
            grid=(blocks // TILE,),
            in_specs=[
                pl.BlockSpec((1, height, columns), lambda g, *_: (0, 0, 0)),
                pl.BlockSpec((HALO, columns), lambda g, *_: (0, 0)),
                pl.BlockSpec((HALO, columns), lambda g, *_: (0, 0)),
                pl.BlockSpec(out_shape, lambda g, *_: (0, 0, 0, 0, 0)),
            ],
            out_specs=(
                pl.BlockSpec((height, wide), lambda g, *_: (0, g)),
                pl.BlockSpec((2, height, wide), lambda g, *_: (0, 0, g)),
                pl.BlockSpec((height, wide), lambda g, *_: (0, g)),
                pl.BlockSpec((2, height, wide), lambda g, *_: (0, 0, g)),
            ),
            scratch_shapes=[pltpu.VMEM((2, 4, height + 2 * HALO, LANES), jnp.float32)],
        ),
    )(where, ratios, potentials, above, below, windows)


def solution(mesh):
    return jax.shard_map(
        per_device,
        mesh=mesh,
        in_specs=(P("cosmo", "row", None), P("cosmo"), P("cosmo"), P("cosmo")),
        out_specs=(
            P(("cosmo", "row"), None),
            P(None, ("cosmo", "row"), None),
            P(("cosmo", "row"), None),
            P(None, ("cosmo", "row"), None),
        ),
        check_vma=False,
    )
```

time: 117 us -> 90.5 us (0.77)
  the two profiles are of different devices: /device:TPU:0 before, /device:TPU:9 now
where the time goes in v2:
time: 90.5 us; the launch traced here: 91.9 us
  Pallas kernels  82.9 us (92%)
  other arithmetic  4.4 us (5%)
  between operations  2.05 us (2%)
  local copies, waits for them, and re-layouts  1.3 us (1%)
  starting transfers between devices  1.28 us (1%)
    pallas_call x1, Pallas kernels, direct(): pl.pallas_call(functools.partial(exchange_kernel, stride, devices, edge_w...  55.9 us
    pallas_call x1, Pallas kernels, per_device(): pl.pallas_call(functools.partial(compute_kernel, blocks), out_shape=(jax....  23 us
    pallas_call x1, Pallas kernels, per_device(): pl.pallas_call(functools.partial(pack_kernel, cap, edge_windows, blocks),...  3.97 us
  transfers between devices with their start and end apart: 1, of which 0 were waited for; matrix products, arithmetic and copies ran while one was open for 3% of the time, Pallas kernels for 0%

profile of v2, /device:TPU:9, one launch (start us, length us, event | category | flops | bytes accessed | tf_op | source)
XLA Modules:
  0.0 91.9 jit_solution(4874071297349223272)
XLA Ops:
  0.6 1.3 %collective-permute-start.7 = (s32[128]{0:T(128)}, s32[128]{0:T(128)S(1)}, u32[]{:S(2)}, u32[]{:S(2)}) collective-permute-start(s32[128]{0:T(128)} %param.12), channel_id=1, source_target_pairs={{0,16},{16,0},{1,17},{17,1},{2,18},{18,2},{3,19},{19,3},{4,20},{20... | collective-permute-start | bytes 1544 | tf_op jit(solution)/shard_map/ppermute | solution.py:21
  1.9 1.3 %slice_bitcast_fusion = (f32[4,16384]{1,0:T(4,128)S(1)}, f32[4,16384]{1,0:T(4,128)S(1)}) fusion(f32[2,16,16384]{2,1,0:T(8,128)} %pot_ref.3), kind=kLoop, calls=%fused_computation.35 | loop fusion | bytes 1048576 | tf_op jit(solution)/shard_map/squeeze | solution.py:234
  3.2 0.0 copy-start
  3.2 0.9 %convert_reduce_fusion.1 = s32[128]{0:T(128)S(1)} fusion(s32[128]{0:T(128)} %param.12), kind=kLoop, calls=%fused_computation.40 | loop fusion | flops 81792 | bytes 1024 | tf_op jit(solution)/shard_map/reduce_sum | solution.py:207
  4.1 0.6 reduce_max.18
  5.4 0.0 collective-permute-done.7
  5.5 0.2 convert_reduce_fusion
  5.6 0.6 reduce_max.19
  6.9 0.7 and_select_fusion.4
  7.7 0.7 select_reduce_fusion.1.src_ref
  8.3 4.0 %shard_map.75 = f32[8,4,34,4,128]{4,3,2,1,0:T(4,128)S(1)} custom-call(s32[256]{0:T(256)} %select_reduce_fusion.1.src_ref, f32[2,16,16384]{2,1,0:T(8,128)} %pot_ref.3), custom_call_target="tpu_custom_call" | custom-call | tf_op jit(solution)/shard_map/pallas_call | solution.py:224
  12.4 0.0 copy-done
  12.4 56.0 %conditional.1 = ((f32[8,6,34,4,128]{4,3,2,1,0:T(4,128)}, f32[4,16384]{1,0:T(4,128)}, f32[4,16384]{1,0:T(4,128)})) conditional(s32[]{:T(128)} %clamp.3, (f32[8,4,34,4,128]{4,3,2,1,0:T(4,128)S(1)}, f32[4,16384]{1,0:T(4,128)S(1)}, f32[4,16384]{1,0:T(4,128)S(1)}) %tuple.26, (f32[8,4,34,4,128]{4,3,2,1,0:T(4,128)S(1)}, ...), branch_computations={%region_5.6_spmd, %region_6.7_spmd, %region_7.8_spmd, %region_8.9_... | conditional | flops 5322496 | bytes 62822200 | solution.py:268
  12.4 55.9 %branch_1_fun.1 = (f32[8,6,34,4,128]{4,3,2,1,0:T(4,128)}, f32[4,16384]{1,0:T(4,128)}, f32[4,16384]{1,0:T(4,128)}) custom-call(f32[8,4,34,4,128]{4,3,2,1,0:T(4,128)S(1)} %get-tuple-element.43.buf_ref, f32[4,16384]{1,0:T(4,128)S(1)} %get-tuple-element.44.top_ref, f32[4,16384]{1,0:T(4,128)S(1)} %get-tuple-element.45.bottom_ref), custom_call_target="tpu_custom_call" | custom-call | tf_op jit(solution)/shard_map/cond/branch_1_fun/pallas_call | solution.py:239
  68.4 0.6 pad_add_fusion.1.where_ref
  69.0 23.0 %shard_map.76 = (f32[16,16384]{1,0:T(8,128)}, f32[2,16,16384]{2,1,0:T(8,128)}, f32[16,16384]{1,0:T(8,128)}, f32[2,16,16384]{2,1,0:T(8,128)}) custom-call(s32[512]{0:T(512)} %pad_add_fusion.1.where_ref, f32[3]{0:T(128)} %ratio_ref.1, f32[2,16,16384]{2,1,0:T(8,128)} %pot_ref.3, f32[4,16384]{1,0:T(4,128)} %get-tuple-element.67.above_ref, ...), custom_call_target="tpu_custom_call" | custom-call | tf_op jit(solution)/shard_map/pallas_call | solution.py:271
  (3 shorter events, 0.1 us)
Async XLA Ops:
  0.6 4.8 %collective-permute-start.7 = (s32[128]{0:T(128)}, s32[128]{0:T(128)S(1)}, u32[]{:S(2)}, u32[]{:S(2)}) collective-permute-start(s32[128]{0:T(128)} %param.12), channel_id=1, source_target_pairs={{0,16},{16,0},{1,17},{17,1},{2,18},{18,2},{3,19},{19,3},{4,20},{20... | collective-permute-start | bytes 1544 | tf_op jit(solution)/shard_map/ppermute | solution.py:21
  3.2 9.2 %copy-start = (s32[128]{0:T(128)S(1)}, s32[128]{0:T(128)}, u32[]{:S(2)}) copy-start(s32[128]{0:T(128)} %param.12) | copy-start | bytes 1540
